TPU v7x, 256 devices: a whole 4x4x8 slice. The times are simulated.
256 devices in a mesh: mat: 4 (over z_lo), tile: 64 (over y, z_hi, x, core).
Axes of the slice: x: 4, y: 4, z: 8 (z_hi: 2, z_lo: 4; z = z_hi * 4 + z_lo), core: 2. Of those that a mesh axis runs over, the one named last changes fastest.
Arguments:
- volume: bfloat16 [4, 512, 64, 1024], P('mat', None, 'tile'), may hold values from -4 to 4
- system: bfloat16 [64, 1024, 32, 128], P('tile'), may hold values from 0 to 0.009521484
- geometry: int32 [64, 16], replicated, may hold values from 0 to 2
- attenuation: float32 [4, 64], replicated, may hold values from 0.05 to 0.5
- response: float32 [8, 64], replicated, may hold values from 0.002 to 0.06
- crosstalk: float32 [8], replicated, may hold values from 0.04 to 0.24
Outputs:
- counts: float32 [8, 512, 16, 512], P(None, ('mat', 'tile'))
Inputs may be any that keep to these rules, and one draw needn't show every extreme that they name: A tile touches, in view v, exactly the 2 detector blocks geometry[t, v] to geometry[t, v] + 1.
All inputs are finite; a program needn't handle non-finite values.
Results may differ from a plain program's by a relative error of at most 0.0003.
Values may be sent and summed in bfloat16 or wider, within the bound.
A program may use at most 128 MiB of HBM per device.

v0:
```python
import jax
import jax.numpy as jnp
from jax import lax
from jax.sharding import PartitionSpec as P

PIXELS = 512
PB = 128
TOUCH = 2
CBINS = 8
SL_DEV = 2
PBLK = 4
KT = 32


def extended(x, sides, width):
    edges = {}
    for axis, dim in sides:
        devices, length = (lax.axis_size(axis), x.shape[dim])
        up = [(i, (i + 1) % devices) for i in range(devices - 1)]
        last = lax.slice_in_dim(x, length - width, length, axis=dim)
        first = lax.slice_in_dim(x, 0, width, axis=dim)
        edges[dim] = (
            lax.ppermute(last, axis, up),
            lax.ppermute(first, axis, [(b, a) for a, b in up]),
        )
    done = []
    for _, dim in sides:
        low, high = edges[dim]
        around = [(width, width) if d in done else (0, 0) for d in range(x.ndim)]
        x = jnp.concatenate([jnp.pad(low, around), x, jnp.pad(high, around)], axis=dim)
        done.append(dim)
    return x


def place_table(first_block, touch_count, block_count):
    touch_ids = jnp.arange(touch_count, dtype=jnp.int32)
    block_ids = jnp.arange(block_count, dtype=jnp.int32)
    return (first_block[..., None, None] + touch_ids[:, None] == block_ids).astype(jnp.float32)


def per_device(volume, system, geometry, attenuation, response, crosstalk):
    mat_count = lax.axis_size("mat")
    tile_count = lax.axis_size("tile")
    slice_count = volume.shape[1]
    tile_vox = volume.shape[3]
    view_count = geometry.shape[1]
    ray_count = view_count * PIXELS
    matrix = system.reshape(tile_vox, KT * PB)
    columns = volume.reshape(mat_count, tile_count, SL_DEV, tile_vox)
    columns = columns.transpose(1, 0, 2, 3).reshape(slice_count, tile_vox)
    row_share = mat_count * SL_DEV
    partial_value = jnp.dot(columns, matrix, preferred_element_type=jnp.float32)
    partial_value = partial_value.reshape(tile_count, row_share, view_count, TOUCH, PB)
    received = lax.all_to_all(partial_value, "tile", split_axis=0, concat_axis=0, tiled=True)
    placed_all = place_table(geometry, TOUCH, PBLK)
    summed = jnp.einsum("qrvjp,qvjb->rvbp", received, placed_all, precision=lax.Precision.HIGHEST)
    summed = summed.reshape(row_share, ray_count)
    integrals = lax.all_to_all(
        summed.reshape(mat_count, SL_DEV, ray_count), "mat", split_axis=0, concat_axis=0, tiled=True
    )
    stacked = integrals.reshape(mat_count, SL_DEV * ray_count)
    exponent = jnp.dot(
        attenuation.T, stacked, preferred_element_type=jnp.float32, precision=lax.Precision.HIGHEST
    )
    detected = jnp.dot(
        response,
        jnp.exp(-exponent),
        preferred_element_type=jnp.float32,
        precision=lax.Precision.HIGHEST,
    )
    detected = detected.reshape(CBINS, SL_DEV, ray_count)
    padded = extended(detected, ((("mat", "tile"), 1),), 1)
    leakage = crosstalk[:, None, None]
    counts = (1.0 - 2.0 * leakage) * detected + leakage * (padded[:, :-2] + padded[:, 2:])
    return counts.reshape(CBINS, SL_DEV, view_count, PIXELS)


def solution(mesh):
    in_specs = (P("mat", None, "tile", None), P("tile", None, None, None), P(), P(), P(), P())
    out_specs = P(None, ("mat", "tile"), None, None)
    return jax.shard_map(
        per_device, mesh=mesh, in_specs=in_specs, out_specs=out_specs, check_vma=False
    )
```

profile of v0, /device:TPU:32, one launch (start us, length us, event | category | flops | bytes accessed | tf_op | source)
XLA Modules:
  0.0 298.2 jit_solution(13730433758599868148)
XLA Ops:
  0.0 0.0 copy-start
  0.0 15.1 %copy.35 = bf16[128,8,32,128]{3,1,2,0:T(8,128)(2,1)} copy(bf16[128,8,32,128]{3,2,1,0:T(8,128)(2,1)} %bitcast.51) | data formatting | bytes 16777216
  15.1 0.0 copy-start.1
  15.1 12.0 %copy.15 = bf16[4096,1024]{1,0:T(8,128)(2,1)} copy(bf16[4096,1024]{0,1:T(8,128)(2,1)} %bitcast.50) | data formatting | bytes 16777216 | tf_op jit(solution)/shard_map/dot_general | solution.py:52
  27.1 0.0 copy-done.1
  27.2 0.4 reshape.32
  27.6 0.3 copy.14
  27.9 7.1 %fusion.13 = f32[64,8,16,2,128]{4,0,3,2,1:T(8,128)S(1)} fusion(bf16[64,8,1024,1,1]{2,0,4,3,1:T(8,128)(2,1)S(1)} %bitcast.59, bf16[16,2,128,1024,1]{3,2,1,0,4:T(8,128)(2,1)} %bitcast.52), kind=kOutput, calls=%fused_computation.18 | convolution fusion | flops 4294967296 | bytes 17825792 | tf_op jit(solution)/shard_map/dot_general | solution.py:52
  34.9 9.8 %copy.16 = f32[64,8,16,2,128]{4,3,1,2,0:T(2,128)} copy(f32[64,8,16,2,128]{4,0,3,2,1:T(8,128)S(1)} %fusion.13) | data formatting | bytes 16777216 | tf_op jit(solution)/shard_map/dot_general | solution.py:52
  44.7 0.0 copy-start.2
  44.7 14.1 %all-to-all-start = ((f32[64,8,16,2,128]{4,3,1,2,0:T(2,128)}), f32[64,8,16,2,128]{4,3,1,2,0:T(2,128)}, u32[]{:S(2)}, u32[]{:S(2)}) async-start(f32[64,8,16,2,128]{4,3,1,2,0:T(2,128)} %copy.16), calls=%async_computation | async-start | bytes 16777216 | tf_op jit(solution)/shard_map/all_to_all | solution.py:54
  58.8 0.0 copy-done.2
  58.8 0.0 copy-start.3
  58.8 0.0 copy-start.4
  58.8 184.5 %all-to-all-done = f32[64,8,16,2,128]{4,3,1,2,0:T(2,128)} async-done(((f32[64,8,16,2,128]{4,3,1,2,0:T(2,128)}), f32[64,8,16,2,128]{4,3,1,2,0:T(2,128)}, u32[]{:S(2)}, u32[]{:S(2)}) %all-to-all-start) | async-done | bytes 8388640 | tf_op jit(solution)/shard_map/all_to_all | solution.py:54
  243.3 10.5 %fusion.3 = f32[8,16,4,128]{3,2,0,1:T(4,128)S(1)} fusion(f32[64,8,16,2,128]{4,3,1,2,0:T(2,128)} %all-to-all-done, s32[64,16,2]{0,2,1:T(2,128)S(1)} %iota_add_fusion), kind=kOutput, calls=%fused_computation.5 | convolution fusion | flops 100671488 | bytes 8658944 | tf_op jit(solution)/shard_map/qrvjp,qvjb->rvbp/dot_general | solution.py:56
  253.8 0.2 reshape_reshape.3
  254.1 16.2 %all_to_all.10 = f32[4,2,8192]{2,1,0:T(2,128)S(1)} all-to-all(f32[4,2,8192]{2,1,0:T(2,128)S(1)} %reshape_reshape.3), channel_id=1, replica_groups=mesh['mat'=4,'tile'=64] {'mat'}, dimensions={0} | all-to-all | bytes 524288 | tf_op jit(solution)/shard_map/all_to_all | solution.py:58
  270.3 0.2 copy.27
  270.5 0.0 copy-done.3
  270.5 3.6 %fusion = f32[16384,64]{0,1:T(8,128)S(1)} fusion(f32[4,16384]{1,0:T(4,128)S(1)} %bitcast.58, f32[4,64]{1,0:T(4,128)S(1)} %copy-done.3), kind=kOutput, calls=%fused_computation.1 | convolution fusion | flops 51380224 | bytes 4457472 | tf_op jit(solution)/shard_map/dot_general | solution.py:62
  274.1 0.0 copy-done
  274.1 2.3 fusion.14
  276.4 1.9 collective-permute-start
  278.3 10.9 %collective-permute-start.1 = (f32[8,1,8192]{2,0,1:T(8,128)S(1)}, f32[8,1,8192]{2,0,1:T(8,128)S(1)}, u32[]{:S(2)}, u32[]{:S(2)}) collective-permute-start(f32[8,1,8192]{2,0,1:T(8,128)S(1)} %get-tuple-element.6), channel_id=1, source_target_pairs={{1,0},{2,1},{3,2},{4,3},{5,4},{6,5},{7,6},{8,7},{9,8},{10,9},{11,1... | collective-permute-start | bytes 786440 | tf_op jit(solution)/shard_map/ppermute | solution.py:24
  289.2 0.0 copy-done.4
  289.2 7.7 %collective-permute-done = f32[8,1,8192]{2,0,1:T(8,128)S(1)} collective-permute-done((f32[8,1,8192]{2,0,1:T(8,128)S(1)}, f32[8,1,8192]{2,0,1:T(8,128)S(1)}, u32[]{:S(2)}, u32[]{:S(2)}) %collective-permute-start) | collective-permute-done | bytes 262176 | tf_op jit(solution)/shard_map/ppermute | solution.py:23
  296.9 0.0 collective-permute-done.1
  296.9 0.2 fusion.8
  297.0 0.3 copy.36
  297.4 0.8 copy.25
  (4 shorter events, 0.1 us)
Async XLA Ops:
  0.0 274.1 %copy-start = (f32[8,64]{1,0:T(8,128)S(1)}, f32[8,64]{1,0:T(8,128)}, u32[]{:S(2)}) copy-start(f32[8,64]{1,0:T(8,128)} %param.10) | copy-start | bytes 6148
  15.1 12.0 %copy-start.1 = (bf16[1,512,1,1024]{3,1,2,0:T(8,128)(2,1)S(1)}, bf16[1,512,1,1024]{3,1,2,0:T(8,128)(2,1)}, u32[]{:S(2)}) copy-start(bf16[1,512,1,1024]{3,1,2,0:T(8,128)(2,1)} %param.6) | copy-start | bytes 3145732
  44.7 14.1 %copy-start.2 = (s32[64,16]{0,1:T(8,128)S(1)}, s32[64,16]{0,1:T(8,128)}, u32[]{:S(2)}) copy-start(s32[64,16]{0,1:T(8,128)} %param.8) | copy-start | bytes 12292
  44.7 198.6 %all-to-all-start = ((f32[64,8,16,2,128]{4,3,1,2,0:T(2,128)}), f32[64,8,16,2,128]{4,3,1,2,0:T(2,128)}, u32[]{:S(2)}, u32[]{:S(2)}) async-start(f32[64,8,16,2,128]{4,3,1,2,0:T(2,128)} %copy.16), calls=%async_computation | async-start | bytes 16777216 | tf_op jit(solution)/shard_map/all_to_all | solution.py:54
  58.8 211.7 %copy-start.3 = (f32[4,64]{1,0:T(4,128)S(1)}, f32[4,64]{1,0:T(4,128)}, u32[]{:S(2)}) copy-start(f32[4,64]{1,0:T(4,128)} %param.9) | copy-start | bytes 3076
  58.8 230.3 %copy-start.4 = (f32[8]{0:T(128)S(1)}, f32[8]{0:T(128)}, u32[]{:S(2)}) copy-start(f32[8]{0:T(128)} %param.11) | copy-start | bytes 100
  276.4 20.5 %collective-permute-start = (f32[8,1,8192]{2,0,1:T(8,128)S(1)}, f32[8,1,8192]{2,0,1:T(8,128)S(1)}, u32[]{:S(2)}, u32[]{:S(2)}) collective-permute-start(f32[8,1,8192]{2,0,1:T(8,128)S(1)} %get-tuple-element.5), channel_id=1, source_target_pairs={{0,1},{1,2},{2,3},{3,4},{4,5},{5,6},{6,7},{7,8},{8,9},{9,10},{10,1... | collective-permute-start | bytes 786440 | tf_op jit(solution)/shard_map/ppermute | solution.py:23
  278.3 18.6 %collective-permute-start.1 = (f32[8,1,8192]{2,0,1:T(8,128)S(1)}, f32[8,1,8192]{2,0,1:T(8,128)S(1)}, u32[]{:S(2)}, u32[]{:S(2)}) collective-permute-start(f32[8,1,8192]{2,0,1:T(8,128)S(1)} %get-tuple-element.6), channel_id=1, source_target_pairs={{1,0},{2,1},{3,2},{4,3},{5,4},{6,5},{7,6},{8,7},{9,8},{10,9},{11,1... | collective-permute-start | bytes 786440 | tf_op jit(solution)/shard_map/ppermute | solution.py:24
where the time goes:
time: 300 us; the launch traced here: 298 us
  waiting for transfers between devices  192 us (64%)
  local copies, waits for them, and re-layouts  39.3 us (13%)
  starting transfers between devices  26.8 us (9%)
  matrix products  23.3 us (8%)
  blocking collectives  16.2 us (5%)
    all_to_all x1, waiting for transfers between devices, per_device(): lax.all_to_all(partial_value, 'tile', split_axis=0, concat_axis=0, tiled=...  184 us
    dot_general x2, local copies, waits for them, and re-layouts, per_device(): partial_value = jnp.dot(columns, matrix, preferred_element_type=jnp.float32)  21.8 us
    all_to_all x1, blocking collectives, per_device(): lax.all_to_all(summed.reshape(mat_count, SL_DEV, ray_count), 'mat', split...  16.2 us
    unnamed x13, local copies, waits for them, and re-layouts  15.6 us
    all_to_all x1, starting transfers between devices, per_device(): lax.all_to_all(partial_value, 'tile', split_axis=0, concat_axis=0, tiled=...  14.1 us
    ppermute x1, starting transfers between devices, extended(): lax.ppermute(first, axis, [(b, a) for a, b in up])  10.9 us
    dot_general x1, matrix products, per_device(): jnp.einsum('qrvjp,qvjb->rvbp', received, placed_all, precision=lax.Precis...  10.5 us
    ppermute x1, waiting for transfers between devices, extended(): lax.ppermute(last, axis, up)  7.71 us
  transfers between devices with their start and end apart: 3, of which 2 were waited for; matrix products, arithmetic and copies ran while one was open for 0% of the time, Pallas kernels for 0%

commit v1 on v0

v1 whole, which is shorter than its diff:
```python
import functools

import jax
import jax.numpy as jnp
from jax import lax
from jax.experimental import pallas as pl
from jax.experimental.pallas import tpu as pltpu
from jax.sharding import PartitionSpec as P

MESH = pl.DeviceIdType.MESH
F32 = jnp.float32
BF16 = jnp.bfloat16
MATS = 4
VOX = 1024
VIEWS = 16
KT = 32
PB = 128
PIX = 512
EBINS = 64
CBINS = 8
SLICES = 512
HALF = SLICES // 2
PAIRS = VIEWS // 2
LOADS = 8
VOX_LOAD = VOX // LOADS
LAG_EXPAND = 1
LAG_RELAY = 2
LAG_OWNER = 3
LAG_CROSS = 4
LAG_DEPTH = 5
LAG_DETECT = 6


def kernel(
    vol_hbm, sys_hbm, geom, att, resp, leak,
    out,
    vol, rows, stage, weights,
    give, keep, take,
    ext, relay, arrive, owned, cross, fbuf,
    zsend, zrecv, proj, hsend, hrecv, obuf,
    load_sem, core_s, core_r, relay_s, relay_r, arrive_s, arrive_r,
    cross_s, cross_r, z_s, z_r, h_s, h_r,
):
    mat = lax.axis_index("mat")
    tile = lax.axis_index("tile")
    core = tile % 2
    x = (tile // 2) % 4
    zh = (tile // 8) % 2
    y = tile // 16
    z = zh * 4 + mat

    def tile_of(yy, zz, xx, cc):
        return ((yy * 2 + zz) * 4 + xx) * 2 + cc

    def x_peer(r):
        return (mat, tile_of(y, zh, (x + r) % 4, core))

    def y_peer(r):
        return (mat, tile_of((y + r) % 4, zh, x, core))

    def z_peer(r):
        zt = (z + r) % 8
        return (zt % 4, tile_of(y, zt // 4, x, core))

    partner = (mat, tile_of(y, zh, x, 1 - core))
    flat = mat * 64 + tile
    after = (flat + 1) % 256
    before = (flat + 255) % 256
    after = (after // 64, after % 64)
    before = (before // 64, before % 64)

    loads = [
        pltpu.make_async_copy(
            sys_hbm.at[pl.ds(n * VOX_LOAD, VOX_LOAD)],
            stage.at[pl.ds(n * VOX_LOAD, VOX_LOAD)],
            load_sem.at[n],
        )
        for n in range(LOADS)
    ]
    vol_load = pltpu.make_async_copy(vol_hbm, vol, load_sem.at[LOADS])
    vol_load.start()
    for load in loads:
        load.start()

    barrier = pltpu.get_barrier_semaphore()
    peers = [partner, after, before]
    peers += [x_peer(r) for r in (1, 2, 3)] + [y_peer(r) for r in (1, 2, 3)]
    peers += [z_peer(r) for r in range(1, 8)]
    for peer in peers:
        pl.semaphore_signal(barrier, inc=1, device_id=peer, device_id_type=MESH)

    r_id = lax.broadcasted_iota(jnp.int32, (SLICES, SLICES), 0)
    s_id = lax.broadcasted_iota(jnp.int32, (SLICES, SLICES), 1)
    r_core = (r_id >> 8) * (2 * core - 1) + (1 - core)
    r_y = ((r_id >> 6) + y) & 3
    r_x = ((r_id >> 4) + x) & 3
    r_mat = (r_id >> 2) & 3
    r_zh = (r_id >> 1) & 1
    want = r_mat * 128 + r_y * 32 + r_zh * 16 + r_x * 4 + r_core * 2 + (r_id & 1)
    order = jnp.where(s_id == want, 1.0, 0.0).astype(BF16)
    vol_load.wait()
    rows[...] = jnp.dot(order, vol[...], preferred_element_type=F32).astype(BF16)

    for n in range(LOADS):
        loads[n].wait()
        for h in range(VOX_LOAD // 64):
            u0 = n * VOX_LOAD + h * 64
            turned = jnp.swapaxes(stage[pl.ds(u0, 64)], 0, 1)
            for k in range(KT):
                weights[k // 2, pl.ds(u0, 64), pl.ds((k % 2) * PB, PB)] = turned[k]

    pl.semaphore_wait(barrier, len(peers))

    def send(src, dst, s, r, peer):
        copy = pltpu.make_async_remote_copy(
            src_ref=src, dst_ref=dst, send_sem=s, recv_sem=r, device_id=peer, device_id_type=MESH
        )
        return copy

    def give_copy(v):
        return send(give.at[v], take.at[v], core_s.at[v], core_r.at[v], partner)

    def chunk(v, u, r, half):
        if u == 0:
            return ext.at[v, pl.ds(half * 2, 2), r]
        return ext.at[v, r, pl.ds(half * 2, 2)]

    first_peer = (x_peer, y_peer)
    second_peer = (y_peer, x_peer)

    def far_copy(v, u, d):
        return send(
            chunk(v, u, 2, d), relay.at[v, d], relay_s.at[v, d], relay_r.at[v, d], first_peer[u]((1, 3)[d])
        )

    def near_copy(v, u, d, half):
        return send(
            chunk(v, u, (1, 3)[d], half),
            arrive.at[v, d, pl.ds(half * 2, 2)],
            arrive_s.at[v, d, half],
            arrive_r.at[v, d, half],
            first_peer[u]((1, 3)[d]),
        )

    def cross_copy(v, u, r):
        return send(
            owned.at[v, r], cross.at[v, r - 1], cross_s.at[v, r - 1], cross_r.at[v, r - 1], second_peer[u](r)
        )

    def z_copy(i, d):
        zt = (z + d) % 8
        q = (zt % 4) * 2 + zt // 4
        return send(
            zsend.at[i, pl.ds(pl.multiple_of(q * 16, 16), 16)],
            zrecv.at[i, z],
            z_s.at[i, d - 1],
            z_r.at[i, d - 1],
            z_peer(d),
        )

    def h_copy(i, d):
        return send(hsend.at[i, d], hrecv.at[i, d], h_s.at[i, d], h_r.at[i, d], (after, before)[d])

    def project(i):
        for u in range(2):
            v = i * 2 + u
            give[v] = jnp.dot(rows[pl.ds(0, HALF)], weights[v], preferred_element_type=F32)
            give_copy(v).start()
        for u in range(2):
            v = i * 2 + u
            keep[v] = jnp.dot(rows[pl.ds(HALF, HALF)], weights[v], preferred_element_type=F32)

    def expand(i):
        for u in range(2):
            v = i * 2 + u
            mine = geom[tile, v]
            theirs = geom[tile + 1 - 2 * core, v]
            give_copy(v).wait_recv()
            for n in range(HALF // 16):
                near = pl.ds(n * 16, 16)
                own0, own1 = keep[v, near, pl.ds(0, PB)], keep[v, near, pl.ds(PB, PB)]
                oth0, oth1 = take[v, near, pl.ds(0, PB)], take[v, near, pl.ds(PB, PB)]
                zero = jnp.zeros_like(own0)
                for b in range(4):
                    total = None
                    for first, part0, part1 in ((mine, own0, own1), (theirs, oth0, oth1)):
                        if b == 0:
                            term = jnp.where(first == 0, part0, zero)
                        elif b == 3:
                            term = jnp.where(first == 2, part1, zero)
                        else:
                            term = jnp.where(first == b, part0, jnp.where(first == b - 1, part1, zero))
                        total = term if total is None else total + term
                    ext[v, n // 4, n % 4, :, pl.ds(b * PB, PB)] = total
            far_copy(v, u, 0).start()
            far_copy(v, u, 1).start()
            near_copy(v, u, 0, 1).start()
            near_copy(v, u, 1, 0).start()

    def pass_on(i):
        for u in range(2):
            v = i * 2 + u
            for d in range(2):
                far_copy(v, u, d).wait_recv()
                target = chunk(v, u, (1, 3)[d], d)
                target[...] = target[...] + relay[v, d]
                near_copy(v, u, d, d).start()

    def gather(i):
        for u in range(2):
            v = i * 2 + u
            for d in range(2):
                for half in range(2):
                    near_copy(v, u, d, half).wait_recv()
            for n in range(4):
                mine = ext[v, n, 0] if u == 0 else ext[v, 0, n]
                owned[v, n] = mine + arrive[v, 0, n] + arrive[v, 1, n]
            for r in (2, 1, 3):
                cross_copy(v, u, r).start()

    def finish(i):
        for u in range(2):
            v = i * 2 + u
            for r in (1, 3, 2):
                cross_copy(v, u, r).wait_recv()
            for b in range(4):
                lanes = pl.ds(b * PB, PB)
                fbuf[u, b] = (owned[v, 0, :, lanes] + cross[v, 0, :, lanes]) + (
                    cross[v, 1, :, lanes] + cross[v, 2, :, lanes]
                )
            for b in range(4):
                for j in range(2):
                    part = fbuf[u, b, pl.ds(j, 8, stride=2), :]
                    zsend[i, pl.ds(u * 8 + j * 4 + b, 8, stride=16), :] = part
        for d in (4, 3, 5, 2, 6, 1, 7):
            z_copy(i, d).start()
        q = mat * 2 + zh
        zrecv[i, z] = zsend[i, pl.ds(pl.multiple_of(q * 16, 16), 16), :]

    sub = lax.broadcasted_iota(jnp.int32, (8, PB), 0)
    low = sub < 4

    def across(i):
        for d in range(1, 8):
            z_copy(i, d).wait_recv()
        for m in range(MATS):
            proj[i, m] = zrecv[i, m] + zrecv[i, 4 + m]
        for u in range(2):
            for p in range(2):
                even = proj[i, 2 * p, pl.ds(u * 8, 8), :]
                odd = proj[i, 2 * p + 1, pl.ds(u * 8, 8), :]
                hsend[i, 0, u, p] = jnp.where(low, pltpu.roll(even, 4, 0), odd)
                hsend[i, 1, u, p] = jnp.where(low, even, pltpu.roll(odd, 4, 0))
        h_copy(i, 0).start()
        h_copy(i, 1).start()

    inside = ((sub >= 4) | (flat > 0)) & ((sub < 4) | (flat < 255))

    def detect(i):
        for d in range(2):
            h_copy(i, d).wait_recv()
        for u in range(2):
            own = [proj[i, m, pl.ds(u * 8, 8), :] for m in range(MATS)]
            side = []
            for p in range(2):
                prev_rows, next_rows = hrecv[i, 0, u, p], hrecv[i, 1, u, p]
                side.append(jnp.where(low, prev_rows, pltpu.roll(next_rows, 4, 0)))
                side.append(jnp.where(low, pltpu.roll(prev_rows, 4, 0), next_rows))

            def energy(e, sums):
                a = [att[m, e] for m in range(MATS)]
                bright = []
                for part in (own, side):
                    level = (a[0] * part[0] + a[1] * part[1]) + (a[2] * part[2] + a[3] * part[3])
                    bright.append(jnp.exp(-level))
                new = []
                for b in range(CBINS):
                    w = resp[b, e]
                    new.append((sums[b][0] + w * bright[0], sums[b][1] + w * bright[1]))
                return tuple(new)

            start = tuple((jnp.zeros((8, PB), F32),) * 2 for _ in range(CBINS))
            sums = lax.fori_loop(0, EBINS, energy, start, unroll=8)
            for b in range(CBINS):
                own_b, side_b = sums[b]
                side_b = jnp.where(inside, side_b, 0.0)
                share = leak[b]
                value = (1.0 - 2.0 * share) * own_b + share * (pltpu.roll(own_b, 4, 0) + side_b)
                obuf[b, pl.ds(i * 2 + u, 8, stride=16), :] = value

    stages = (
        (0, project), (LAG_EXPAND, expand), (LAG_RELAY, pass_on), (LAG_OWNER, gather),
        (LAG_CROSS, finish), (LAG_DEPTH, across), (LAG_DETECT, detect),
    )

    def step(t, carry):
        for lag, run in stages:
            i = t - lag

            @pl.when((i >= 0) & (i < PAIRS))
            def _(i=i, run=run):
                run(i)

        return carry

    lax.fori_loop(0, PAIRS + LAG_DETECT, step, 0)

    for j in range(2):
        for b in range(4):
            out[:, j, :, pl.ds(b * PB, PB)] = obuf[:, pl.ds((j * 4 + b) * 16, 16), :]

    def drain(i, carry):
        for u in range(2):
            v = i * 2 + u
            give_copy(v).wait_send()
            for d in range(2):
                far_copy(v, u, d).wait_send()
                for half in range(2):
                    near_copy(v, u, d, half).wait_send()
            for r in (1, 2, 3):
                cross_copy(v, u, r).wait_send()
        for d in range(1, 8):
            z_copy(i, d).wait_send()
        for d in range(2):
            h_copy(i, d).wait_send()
        return carry

    lax.fori_loop(0, PAIRS, drain, 0)


def per_device(volume, system, geometry, attenuation, response, crosstalk):
    dma = pltpu.SemaphoreType.DMA
    vmem = pltpu.VMEM
    smem = pl.BlockSpec(memory_space=pltpu.SMEM)
    far = pl.BlockSpec(memory_space=pl.ANY)
    return pl.pallas_call(
        kernel,
        out_shape=jax.ShapeDtypeStruct((CBINS, 2, VIEWS, PIX), F32),
        in_specs=[far, far, smem, smem, smem, smem],
        out_specs=pl.BlockSpec(memory_space=pltpu.VMEM),
        scratch_shapes=[
            vmem((SLICES, VOX), BF16),
            vmem((SLICES, VOX), BF16),
            vmem((VOX, KT, PB), BF16),
            vmem((VIEWS, VOX, 2 * PB), BF16),
            vmem((VIEWS, HALF, 2 * PB), F32),
            vmem((VIEWS, HALF, 2 * PB), F32),
            vmem((VIEWS, HALF, 2 * PB), F32),
            vmem((VIEWS, 4, 4, 16, PIX), F32),
            vmem((VIEWS, 2, 2, 16, PIX), F32),
            vmem((VIEWS, 2, 4, 16, PIX), F32),
            vmem((VIEWS, 4, 16, PIX), F32),
            vmem((VIEWS, 3, 16, PIX), F32),
            vmem((2, 4, 16, PB), F32),
            vmem((PAIRS, 128, PB), F32),
            vmem((PAIRS, 8, 16, PB), F32),
            vmem((PAIRS, MATS, 16, PB), F32),
            vmem((PAIRS, 2, 2, 2, 8, PB), F32),
            vmem((PAIRS, 2, 2, 2, 8, PB), F32),
            vmem((CBINS, 128, PB), F32),
            dma((LOADS + 1,)),
            dma((VIEWS,)),
            dma((VIEWS,)),
            dma((VIEWS, 2)),
            dma((VIEWS, 2)),
            dma((VIEWS, 2, 2)),
            dma((VIEWS, 2, 2)),
            dma((VIEWS, 3)),
            dma((VIEWS, 3)),
            dma((PAIRS, 7)),
            dma((PAIRS, 7)),
            dma((PAIRS, 2)),
            dma((PAIRS, 2)),
        ],
        compiler_params=pltpu.CompilerParams(
            collective_id=0, has_side_effects=True, vmem_limit_bytes=67043328
        ),
    )(
        volume.reshape(SLICES, VOX),
        system.reshape(VOX, KT, PB),
        geometry,
        attenuation,
        response,
        crosstalk,
    )


def solution(mesh):
    in_specs = (P("mat", None, "tile", None), P("tile", None, None, None), P(), P(), P(), P())
    out_specs = P(None, ("mat", "tile"), None, None)
    return jax.shard_map(
        per_device, mesh=mesh, in_specs=in_specs, out_specs=out_specs, check_vma=False
    )
```

time: 300 us -> 88 us (0.29)
  waiting for transfers between devices: 192 us -> 0 us
  Pallas kernels: 0 us -> 84.4 us
  local copies, waits for them, and re-layouts: 39.3 us -> 3.27 us
  starting transfers between devices: 26.8 us -> 0 us
  matrix products: 23.3 us -> 0 us
  blocking collectives: 16.2 us -> 0 us
    all_to_all x1 -> x0, waiting for transfers between devices: 184 us -> none  [per_device(): lax.all_to_all(partial_value, 'tile', split_axis=0, concat_axis=0, tiled=...]
    pallas_call x0 -> x1, Pallas kernels: none -> 84.4 us  [per_device(): pl.pallas_call(kernel, out_shape=jax.ShapeDtypeStruct((CBINS, 2, VIEWS, P...]
    dot_general x4 -> x0, matrix products: 23.3 us -> none  [the longest x1 10.5 us: per_device(): jnp.einsum('qrvjp,qvjb->rvbp', received, placed_all, precision=lax.Precis...]
    dot_general x2 -> x0, local copies, waits for them, and re-layouts: 21.8 us -> none  [per_device(): partial_value = jnp.dot(columns, matrix, preferred_element_type=jnp.float32)]
    all_to_all x1 -> x0, blocking collectives: 16.2 us -> none  [per_device(): lax.all_to_all(summed.reshape(mat_count, SL_DEV, ray_count), 'mat', split...]
    all_to_all x1 -> x0, starting transfers between devices: 14.1 us -> none  [per_device(): lax.all_to_all(partial_value, 'tile', split_axis=0, concat_axis=0, tiled=...]
    ppermute x2 -> x0, starting transfers between devices: 12.8 us -> none  [the longest x1 10.9 us: extended(): lax.ppermute(first, axis, [(b, a) for a, b in up])]
    unnamed x13 -> x2, local copies, waits for them, and re-layouts: 15.6 us -> 3.27 us
  transfers between devices with their start and end apart: 3 -> 0, of which waited for: 2 -> 0; matrix products, arithmetic and copies ran while one was open for 0% -> 0% of each run, Pallas kernels for 0% -> 0%
where the time goes in v1:
time: 88 us; the launch traced here: 87.7 us
  Pallas kernels  84.4 us (96%)
  local copies, waits for them, and re-layouts  3.27 us (4%)
    pallas_call x1, Pallas kernels, per_device(): pl.pallas_call(kernel, out_shape=jax.ShapeDtypeStruct((CBINS, 2, VIEWS, P...  84.4 us
    unnamed x2, local copies, waits for them, and re-layouts  3.27 us

profile of v1, /device:TPU:32, one launch (start us, length us, event | category | flops | bytes accessed | tf_op | source)
XLA Modules:
  0.0 87.7 jit_solution(16012767068246553359)
XLA Ops:
  0.0 1.4 %copy.7.geom = s32[64,16]{1,0:T(8,128)} copy(s32[64,16]{0,1:T(8,128)} %param.8) | data formatting | bytes 8192 | tf_op args[2]
  1.4 84.4 %shard_map.64 = f32[8,2,16,512]{3,2,1,0:T(8,128)} custom-call(bf16[512,1024]{1,0:T(8,128)(2,1)} %bitcast.3, bf16[1024,32,128]{2,1,0:T(8,128)(2,1)} %bitcast.2, s32[64,16]{1,0:T(8,128)} %copy.7.geom, f32[4,64]{1,0:T(4,128)} %att.1, f32[8,64]{1,0:T(8,128)} %resp.1, f32[8]{0:T(128)} %leak.1), custom_call_target="tpu_custom_call" | custom-call | tf_op jit(solution)/shard_map/pallas_call | solution.py:336
  85.8 1.9 %copy.9 = f32[8,2,16,512]{3,2,1,0:T(8,128)} copy(f32[8,2,16,512]{3,2,1,0:T(8,128)} %shard_map.64) | data formatting | bytes 1048576

commit v2 on v1

v2 whole, which is shorter than its diff:
```python
import functools

import jax
import jax.numpy as jnp
from jax import lax
from jax.experimental import pallas as pl
from jax.experimental.pallas import tpu as pltpu
from jax.sharding import PartitionSpec as P

MESH = pl.DeviceIdType.MESH
F32 = jnp.float32
BF16 = jnp.bfloat16
I32 = jnp.int32
TOP = 32767
LOG2E = 1.4426950408889634
MIX_ATT = (0, 1, 2, 0, 1, 0)
MIX_PROJ = (0, 0, 0, 1, 1, 2)
MATS = 4
VOX = 1024
VIEWS = 16
KT = 32
PB = 128
PIX = 512
EBINS = 64
CBINS = 8
SLICES = 512
HALF = SLICES // 2
PAIRS = VIEWS // 2
KG = 8
GROUPS = KT // KG
LAG_EXPAND = 1
LAG_RELAY = 2
LAG_OWNER = 3
LAG_CROSS = 4
LAG_DETECT = 6
LAG_COMBINE = 8
OPITCH = 24


def kernel(
    vol_hbm, sys_hbm, geom, att, resp, leak,
    out,
    vol, rows, stage, weights,
    give, keep, take,
    ext, far_out, far_in, near_out, near_in, size_out, size_in,
    owned, cross_out, cross_in, csize_out, csize_in,
    zsort, zsend, zrecv, proj, att_mix, resp_mix, shine, hrecv, obuf,
    load_sem, core_s, core_r, far_s, far_r, near_s, near_r, size_s, size0_r, size1_r,
    cross_s, cross_r, csize_s, csize_r, z_s, z_r, h_s, h_r,
):
    mat = lax.axis_index("mat")
    tile = lax.axis_index("tile")
    core = tile % 2
    x = (tile // 2) % 4
    zh = (tile // 8) % 2
    y = tile // 16
    z = zh * 4 + mat

    def tile_of(yy, zz, xx, cc):
        return ((yy * 2 + zz) * 4 + xx) * 2 + cc

    def x_peer(r):
        return (mat, tile_of(y, zh, (x + r) % 4, core))

    def y_peer(r):
        return (mat, tile_of((y + r) % 4, zh, x, core))

    def z_peer(r):
        zt = (z + r) % 8
        return (zt % 4, tile_of(y, zt // 4, x, core))

    partner = (mat, tile_of(y, zh, x, 1 - core))
    flat = mat * 64 + tile
    after = (flat + 1) % 256
    before = (flat + 255) % 256
    after = (after // 64, after % 64)
    before = (before // 64, before % 64)

    vol_load = pltpu.make_async_copy(vol_hbm, vol, load_sem.at[GROUPS])
    vol_load.start()
    loads = [
        pltpu.make_async_copy(sys_hbm.at[:, pl.ds(g * KG, KG)], stage.at[g], load_sem.at[g])
        for g in range(GROUPS)
    ]
    for load in loads:
        load.start()

    def parts_of(value):
        first = value.astype(BF16)
        rest = value - first.astype(F32)
        second = rest.astype(BF16)
        return first, second, (rest - second.astype(F32)).astype(BF16)

    def iota(shape, axis):
        return lax.broadcasted_iota(I32, shape, axis)

    def mixers():
        wide = len(MIX_ATT) * 32
        column = iota((MATS, wide), 1)
        pick = ((column >> 3) & 3) == iota((MATS, wide), 0)
        level = None
        for p, part in enumerate(parts_of(att[...] * (-LOG2E))):
            chosen = None
            for n, q in enumerate(MIX_ATT):
                if q == p:
                    here = (column >> 5) == n
                    chosen = here if chosen is None else chosen | here
            select = jnp.where(pick & chosen, 1.0, 0.0).astype(BF16)
            term = lax.dot_general(
                part, select, (((0,), (0,)), ((), ())), preferred_element_type=F32
            )
            level = term if level is None else level + term
        ray = iota((EBINS, wide), 1) & 7
        for n in range(8):
            att_mix[pl.ds(n * EBINS, EBINS), :] = jnp.where(ray == n, level, 0.0).astype(BF16)
        spread = jnp.where((iota((EBINS, 256), 1) & 63) == iota((EBINS, 256), 0), 1.0, 0.0)
        block = iota((CBINS, 256), 1) >> 6
        for p, part in enumerate(parts_of(resp[...])[:2]):
            flat_part = jnp.dot(part, spread.astype(BF16), preferred_element_type=F32)
            tall = [jnp.where(block == n, flat_part, 0.0) for n in range(4)]
            resp_mix[pl.ds(p * 32, 32), :] = jnp.concatenate(tall, axis=0).astype(BF16)

    barrier = pltpu.get_barrier_semaphore()
    peers = [partner, after, before]
    peers += [x_peer(r) for r in (1, 2, 3)] + [y_peer(r) for r in (1, 2, 3)]
    peers += [z_peer(r) for r in range(1, 8)]
    for peer in peers:
        pl.semaphore_signal(barrier, inc=1, device_id=peer, device_id_type=MESH)

    r_id = lax.broadcasted_iota(jnp.int32, (SLICES, SLICES), 0)
    s_id = lax.broadcasted_iota(jnp.int32, (SLICES, SLICES), 1)
    r_core = (r_id >> 8) * (2 * core - 1) + (1 - core)
    r_y = ((r_id >> 6) + y) & 3
    r_x = ((r_id >> 4) + x) & 3
    r_mat = (r_id >> 2) & 3
    r_zh = (r_id >> 1) & 1
    want = r_mat * 128 + r_y * 32 + r_zh * 16 + r_x * 4 + r_core * 2 + (r_id & 1)
    order = jnp.where(s_id == want, 1.0, 0.0).astype(BF16)
    mixers()
    vol_load.wait()
    loads[0].wait()
    rows[...] = jnp.dot(order, vol[...], preferred_element_type=F32).astype(BF16)

    def turn_block(g, n):
        near = pl.ds(n * 128, 128)
        turned = jnp.swapaxes(stage[g, near], 0, 1)
        for k in range(KG):
            weights[g * (KG // 2) + k // 2, near, pl.ds((k % 2) * PB, PB)] = turned[k]

    for n in range(VOX // 128):
        turn_block(0, n)
    pl.semaphore_wait(barrier, len(peers))

    def turn(g):
        pltpu.make_async_copy(
            sys_hbm.at[:, pl.ds(pl.multiple_of(g * KG, KG), KG)], stage.at[g], load_sem.at[g]
        ).wait()
        for n in range(VOX // 128):
            turn_block(g, n)

    def send(src, dst, s, r, peer):
        copy = pltpu.make_async_remote_copy(
            src_ref=src, dst_ref=dst, send_sem=s, recv_sem=r, device_id=peer, device_id_type=MESH
        )
        return copy

    def give_copy(v):
        return send(give.at[v], take.at[v], core_s, core_r.at[v // 2], partner)

    def await_all(ref, sem):
        pltpu.make_async_copy(ref, ref, sem).wait()

    def chunk(v, u, r, half):
        if u == 0:
            return ext.at[v, pl.ds(half * 2, 2), r]
        return ext.at[v, r, pl.ds(half * 2, 2)]

    first_peer = (x_peer, y_peer)
    second_peer = (y_peer, x_peer)

    def far_copy(v, u, d):
        return send(far_out.at[v, d], far_in.at[v, d], far_s, far_r.at[v // 2], first_peer[u]((1, 3)[d]))

    def near_copy(v, u, d, late):
        return send(
            near_out.at[v, d, late], near_in.at[v, d, late], near_s, near_r.at[v // 2], first_peer[u]((1, 3)[d])
        )

    def size_copy(v, u, d, late):
        return send(
            size_out.at[late, v, d], size_in.at[late, v, d],
            size_s, (size0_r, size1_r)[late].at[v // 2], first_peer[u]((1, 3)[d]),
        )

    def cross_copy(v, u, r):
        return send(
            cross_out.at[v, r - 1], cross_in.at[v, r - 1], cross_s, cross_r.at[v // 2], second_peer[u](r)
        )

    def csize_copy(v, u, r):
        return send(
            csize_out.at[v, r - 1], csize_in.at[v, r - 1], csize_s, csize_r.at[v // 2], second_peer[u](r)
        )

    def peak(parts):
        top = None
        for part in parts:
            part = jnp.abs(part)
            top = part if top is None else jnp.maximum(top, part)
        return jnp.max(top, axis=0, keepdims=True)

    def code(first, second, inverse):
        first = jnp.round(first * inverse).astype(I32)
        second = jnp.round(second * inverse).astype(I32)
        return (first << 16) + second

    def inverse_of(top):
        return TOP / jnp.maximum(top, 1e-30)

    def decode(word, unit):
        first = (word + 32768) >> 16
        second = word - (first << 16)
        return first.astype(F32) * unit, second.astype(F32) * unit

    def lanes(b):
        return pl.ds(b * PB, PB)

    def z_copy(i, d):
        zt = (z + d) % 8
        q = (zt % 4) * 2 + zt // 4
        return send(
            zsend.at[i, pl.ds(pl.multiple_of(q * 16, 16), 16)],
            zrecv.at[i, z],
            z_s,
            z_r.at[i],
            z_peer(d),
        )

    def h_copy(i, d):
        return send(shine.at[i, 1 - d], hrecv.at[i, d], h_s, h_r.at[i], (after, before)[d])

    def both_views(i):
        return pl.ds(i * 2, 2)

    def project(i):
        for u in range(2):
            v = i * 2 + u
            both = jnp.dot(rows[...], weights[v], preferred_element_type=F32)
            give[v] = both[:HALF]
            give_copy(v).start()
            keep[v] = both[HALF:]

    def expand(i):
        await_all(take.at[both_views(i)], core_r.at[i])
        for u in range(2):
            v = i * 2 + u
            mine = geom[v, tile]
            theirs = geom[v, tile + 1 - 2 * core]
            for n in range(HALF // 16):
                near = pl.ds(n * 16, 16)
                own0, own1 = keep[v, near, pl.ds(0, PB)], keep[v, near, pl.ds(PB, PB)]
                oth0, oth1 = take[v, near, pl.ds(0, PB)], take[v, near, pl.ds(PB, PB)]
                zero = jnp.zeros_like(own0)
                for b in range(4):
                    total = None
                    for first, part0, part1 in ((mine, own0, own1), (theirs, oth0, oth1)):
                        if b == 0:
                            term = jnp.where(first == 0, part0, zero)
                        elif b == 3:
                            term = jnp.where(first == 2, part1, zero)
                        else:
                            term = jnp.where(first == b, part0, jnp.where(first == b - 1, part1, zero))
                        total = term if total is None else total + term
                    ext[v, n // 4, n % 4, :, lanes(b)] = total
            for d in range(2):
                far, near = chunk(v, u, 2, d), chunk(v, u, (1, 3)[d], 1 - d)
                top = peak(
                    part[n, :, lanes(b)] for part in (far, near) for n in range(2) for b in range(4)
                )
                size_out[0, v, d] = top * (1.0 / TOP)
                inverse = inverse_of(top)
                for b in range(4):
                    far_out[v, d, :, lanes(b)] = code(far[0, :, lanes(b)], far[1, :, lanes(b)], inverse)
                size_copy(v, u, d, 0).start()
                far_copy(v, u, d).start()
                for b in range(4):
                    near_out[v, d, 0, :, lanes(b)] = code(near[0, :, lanes(b)], near[1, :, lanes(b)], inverse)
                near_copy(v, u, d, 0).start()

    def pass_on(i):
        await_all(size_in.at[0, both_views(i)], size0_r.at[i])
        await_all(far_in.at[both_views(i)], far_r.at[i])
        for u in range(2):
            v = i * 2 + u
            for d in range(2):
                unit = size_in[0, v, d]
                mine = chunk(v, u, (1, 3)[d], d)
                sums = []
                for b in range(4):
                    first, second = decode(far_in[v, d, :, lanes(b)], unit)
                    sums.append((mine[0, :, lanes(b)] + first, mine[1, :, lanes(b)] + second))
                top = peak(part for both in sums for part in both)
                size_out[1, v, d] = top * (1.0 / TOP)
                inverse = inverse_of(top)
                for b in range(4):
                    near_out[v, d, 1, :, lanes(b)] = code(sums[b][0], sums[b][1], inverse)
                size_copy(v, u, d, 1).start()
                near_copy(v, u, d, 1).start()

    def gather(i):
        await_all(size_in.at[1, both_views(i)], size1_r.at[i])
        await_all(near_in.at[both_views(i)], near_r.at[i])
        for u in range(2):
            v = i * 2 + u
            units = [[size_in[late, v, d] for late in range(2)] for d in range(2)]
            total = [[None] * 4 for _ in range(4)]
            for half in range(2):
                for b in range(4):
                    up = decode(near_in[v, 0, 1 - half, :, lanes(b)], units[0][1 - half])
                    down = decode(near_in[v, 1, half, :, lanes(b)], units[1][half])
                    for k in range(2):
                        n = half * 2 + k
                        mine = ext[v, n, 0, :, lanes(b)] if u == 0 else ext[v, 0, n, :, lanes(b)]
                        total[n][b] = mine + (up[k] + down[k])
            for b in range(4):
                owned[v, :, lanes(b)] = total[0][b]
            for r in (2, 1, 3):
                top = peak(total[r][b][8 * k : 8 * k + 8] for b in range(4) for k in range(2))
                csize_out[v, r - 1] = top * (1.0 / TOP)
                inverse = inverse_of(top)
                for b in range(4):
                    cross_out[v, r - 1, :, lanes(b)] = code(total[r][b][:8], total[r][b][8:], inverse)
                csize_copy(v, u, r).start()
                cross_copy(v, u, r).start()

    def finish(i):
        await_all(csize_in.at[both_views(i)], csize_r.at[i])
        await_all(cross_in.at[both_views(i)], cross_r.at[i])
        for u in range(2):
            v = i * 2 + u
            units = [csize_in[v, r] for r in range(3)]
            for b in range(4):
                got = [decode(cross_in[v, r, :, lanes(b)], units[r]) for r in range(3)]
                for k in range(2):
                    part = owned[v, pl.ds(8 * k, 8), lanes(b)] + (got[0][k] + (got[1][k] + got[2][k]))
                    zsort[u, pl.ds(32 * k + b, 8, stride=4), :] = part
            for q in range(8):
                zsend[i, pl.ds(q * 16 + u * 8, 8), :] = zsort[u, pl.ds(q * 8, 8), :]
        for d in (4, 3, 5, 2, 6, 1, 7):
            z_copy(i, d).start()
        q = mat * 2 + zh
        zrecv[i, z] = zsend[i, pl.ds(pl.multiple_of(q * 16, 16), 16), :]

    def detect(i):
        await_all(zrecv.at[i, pl.ds(0, 7)], z_r.at[i])
        for m in range(MATS):
            both = zrecv[i, m] + zrecv[i, 4 + m]
            for u in range(2):
                proj[pl.ds(m * 8, 8), pl.ds(u * PB, PB)] = both[u * 8 : u * 8 + 8]
        parts = parts_of(proj[...])
        mixed = jnp.concatenate([parts[p] for p in MIX_PROJ], axis=0)
        for j in range(2):
            level = jnp.dot(att_mix[pl.ds(j * 256, 256), :], mixed, preferred_element_type=F32)
            bright = jnp.exp2(level)
            first = bright.astype(BF16)
            second = (bright - first.astype(F32)).astype(BF16)
            large = jnp.dot(resp_mix[...], first, preferred_element_type=F32)
            small = jnp.dot(resp_mix[pl.ds(0, 32), :], second, preferred_element_type=F32)
            shine[i, j] = large[:32] + (large[32:] + small)
        h_copy(i, 0).start()
        h_copy(i, 1).start()

    share = jnp.zeros((CBINS, PB), F32)
    for n in range(CBINS):
        share = jnp.where(iota((CBINS, PB), 0) == n, leak[n], share)
    rest = 1.0 - 2.0 * share
    outer = (flat > 0, flat < 255)

    def combine(i):
        await_all(hrecv.at[i], h_r.at[i])
        for b in range(4):
            near = pl.ds(b * 8, 8)
            own = [shine[i, j, near, :] for j in range(2)]
            for j in range(2):
                side = jnp.where(outer[j], hrecv[i, j, near, :], 0.0)
                for u in range(2):
                    half = slice(u * PB, u * PB + PB)
                    value = rest * own[j][:, half] + share * (own[1 - j][:, half] + side[:, half])
                    obuf[j * 4 + b, pl.ds(i * 2 + u, 8, stride=OPITCH), :] = value

    stages = (
        (0, project), (LAG_EXPAND, expand), (LAG_RELAY, pass_on), (LAG_OWNER, gather),
        (LAG_CROSS, finish), (LAG_DETECT, detect), (LAG_COMBINE, combine),
    )

    def step(t, carry):
        for lag, run in stages:
            i = t - lag

            @pl.when((i >= 0) & (i < PAIRS))
            def _(i=i, run=run):
                run(i)

            if run is project:
                g = (t // 2) + 1

                @pl.when((t % 2 == 0) & (g < GROUPS))
                def _(g=g):
                    turn(g)

        return carry

    lax.fori_loop(0, PAIRS + LAG_COMBINE, step, 0)

    for j in range(2):
        for b in range(4):
            for n in range(CBINS):
                out[n, j, :, lanes(b)] = obuf[j * 4 + b, pl.ds(n * OPITCH, VIEWS), :]

    for ref, sem in (
        (give, core_s), (far_out, far_s), (near_out, near_s), (size_out, size_s), (cross_out, cross_s),
        (csize_out, csize_s), (zsend.at[:, pl.ds(0, 112)], z_s), (shine, h_s),
    ):
        await_all(ref, sem)


def per_device(volume, system, geometry, attenuation, response, crosstalk):
    dma = pltpu.SemaphoreType.DMA
    vmem = pltpu.VMEM
    smem = pl.BlockSpec(memory_space=pltpu.SMEM)
    far = pl.BlockSpec(memory_space=pl.ANY)
    near = pl.BlockSpec(memory_space=pltpu.VMEM)
    return pl.pallas_call(
        kernel,
        out_shape=jax.ShapeDtypeStruct((CBINS, 2, VIEWS, PIX), F32),
        in_specs=[far, far, smem, near, near, smem],
        out_specs=pl.BlockSpec(memory_space=pltpu.VMEM),
        scratch_shapes=[
            vmem((SLICES, VOX), BF16),
            vmem((SLICES, VOX), BF16),
            vmem((GROUPS, VOX, KG, PB), BF16),
            vmem((VIEWS, VOX, 2 * PB), BF16),
            vmem((VIEWS, HALF, 2 * PB), F32),
            vmem((VIEWS, HALF, 2 * PB), F32),
            vmem((VIEWS, HALF, 2 * PB), F32),
            vmem((VIEWS, 4, 4, 16, PIX), F32),
            vmem((VIEWS, 2, 16, PIX), I32),
            vmem((VIEWS, 2, 16, PIX), I32),
            vmem((VIEWS, 2, 2, 16, PIX), I32),
            vmem((VIEWS, 2, 2, 16, PIX), I32),
            vmem((2, VIEWS, 2, 1, PB), F32),
            vmem((2, VIEWS, 2, 1, PB), F32),
            vmem((VIEWS, 16, PIX), F32),
            vmem((VIEWS, 3, 8, PIX), I32),
            vmem((VIEWS, 3, 8, PIX), I32),
            vmem((VIEWS, 3, 1, PB), F32),
            vmem((VIEWS, 3, 1, PB), F32),
            vmem((2, 64, PB), F32),
            vmem((PAIRS, 128, PB), F32),
            vmem((PAIRS, 8, 16, PB), F32),
            vmem((32, 2 * PB), F32),
            vmem((8 * EBINS, len(MIX_ATT) * 32), BF16),
            vmem((64, 256), BF16),
            vmem((PAIRS, 2, 32, 2 * PB), F32),
            vmem((PAIRS, 2, 32, 2 * PB), F32),
            vmem((8, CBINS * OPITCH, PB), F32),
            dma((GROUPS + 1,)),
            dma, dma((PAIRS,)),
            dma, dma((PAIRS,)),
            dma, dma((PAIRS,)),
            dma, dma((PAIRS,)), dma((PAIRS,)),
            dma, dma((PAIRS,)),
            dma, dma((PAIRS,)),
            dma, dma((PAIRS,)),
            dma, dma((PAIRS,)),
        ],
        compiler_params=pltpu.CompilerParams(
            collective_id=0, has_side_effects=True, vmem_limit_bytes=67043328
        ),
    )(
        volume.reshape(SLICES, VOX),
        system.reshape(VOX, KT, PB),
        geometry.T,
        attenuation,
        response,
        crosstalk,
    )


def solution(mesh):
    in_specs = (P("mat", None, "tile", None), P("tile", None, None, None), P(), P(), P(), P())
    out_specs = P(None, ("mat", "tile"), None, None)
    return jax.shard_map(
        per_device, mesh=mesh, in_specs=in_specs, out_specs=out_specs, check_vma=False
    )
```

time: 88 us -> 64.7 us (0.74)
  Pallas kernels: 84.4 us -> 62.6 us
  local copies, waits for them, and re-layouts: 3.27 us -> 1.88 us
    pallas_call x1, Pallas kernels: 84.4 us -> 62.6 us  [per_device(): pl.pallas_call(kernel, out_shape=jax.ShapeDtypeStruct((CBINS, 2, VIEWS, P...]
    unnamed x2 -> x1, local copies, waits for them, and re-layouts: 3.27 us -> 1.88 us
where the time goes in v2:
time: 64.7 us; the launch traced here: 64.5 us
  Pallas kernels  62.6 us (97%)
  local copies, waits for them, and re-layouts  1.88 us (3%)
    pallas_call x1, Pallas kernels, per_device(): pl.pallas_call(kernel, out_shape=jax.ShapeDtypeStruct((CBINS, 2, VIEWS, P...  62.6 us
    unnamed x1, local copies, waits for them, and re-layouts  1.88 us

profile of v2, /device:TPU:32, one launch (start us, length us, event | category | flops | bytes accessed | tf_op | source)
XLA Modules:
  0.0 64.5 jit_solution(5130285028355921722)
XLA Ops:
  0.0 62.6 %shard_map.64 = f32[8,2,16,512]{3,2,1,0:T(8,128)} custom-call(bf16[512,1024]{1,0:T(8,128)(2,1)} %bitcast.4, bf16[1024,32,128]{2,1,0:T(8,128)(2,1)} %bitcast.3, s32[16,64]{1,0:T(8,128)} %bitcast.5, f32[4,64]{1,0:T(4,128)} %att.1, f32[8,64]{1,0:T(8,128)} %resp.1, f32[8]{0:T(128)} %leak.1), custom_call_target="tpu_custom_call" | custom-call | tf_op jit(solution)/shard_map/pallas_call | solution.py:433
  62.6 1.9 %copy.8 = f32[8,2,16,512]{3,2,1,0:T(8,128)} copy(f32[8,2,16,512]{3,2,1,0:T(8,128)} %shard_map.64) | data formatting | bytes 1048576

commit v3 on v2

--- a/solution.py
+++ b/solution.py
@@ -28,13 +28,16 @@
 PAIRS = VIEWS // 2
 KG = 8
 GROUPS = KT // KG
-LAG_EXPAND = 1
-LAG_RELAY = 2
-LAG_OWNER = 3
-LAG_CROSS = 4
-LAG_DETECT = 6
-LAG_COMBINE = 8
+LAG_PROJECT = -2
+LAG_EXPAND = -1
+LAG_RELAY = 1
+LAG_OWNER = 2
+LAG_CROSS = 3
+LAG_DETECT = 5
+LAG_COMBINE = 7
+MERGE = 2
 OPITCH = 24
+DIRECT = 2
 
 
 def kernel(
@@ -44,9 +47,9 @@
     give, keep, take,
     ext, far_out, far_in, near_out, near_in, size_out, size_in,
     owned, cross_out, cross_in, csize_out, csize_in,
-    zsort, zsend, zrecv, proj, att_mix, resp_mix, shine, hrecv, obuf,
+    zsort, zsend, zrecv, proj, att_mix, resp_mix, shine, hrecv, obuf, hz_out, hz_in, aside,
     load_sem, core_s, core_r, far_s, far_r, near_s, near_r, size_s, size0_r, size1_r,
-    cross_s, cross_r, csize_s, csize_r, z_s, z_r, h_s, h_r,
+    cross_s, cross_r, csize_s, csize_r, z_s, z_r, h_s, h_r, hz_s, hz_r, met,
 ):
     mat = lax.axis_index("mat")
     tile = lax.axis_index("tile")
@@ -71,10 +74,12 @@
 
     partner = (mat, tile_of(y, zh, x, 1 - core))
     flat = mat * 64 + tile
-    after = (flat + 1) % 256
-    before = (flat + 255) % 256
-    after = (after // 64, after % 64)
-    before = (before // 64, before % 64)
+
+    def beside(where, d):
+        other = (where + (1, 255)[d]) % 256
+        return other // 64, other % 64
+
+    after, before = beside(flat, 0), beside(flat, 1)
 
     vol_load = pltpu.make_async_copy(vol_hbm, vol, load_sem.at[GROUPS])
     vol_load.start()
@@ -127,19 +132,22 @@
     for peer in peers:
         pl.semaphore_signal(barrier, inc=1, device_id=peer, device_id_type=MESH)
 
-    r_id = lax.broadcasted_iota(jnp.int32, (SLICES, SLICES), 0)
-    s_id = lax.broadcasted_iota(jnp.int32, (SLICES, SLICES), 1)
-    r_core = (r_id >> 8) * (2 * core - 1) + (1 - core)
-    r_y = ((r_id >> 6) + y) & 3
+    r_id, s_id = iota((128, 128), 0), iota((128, 128), 1)
+    r_core = (r_id >> 6) * (2 * core - 1) + (1 - core)
     r_x = ((r_id >> 4) + x) & 3
-    r_mat = (r_id >> 2) & 3
-    r_zh = (r_id >> 1) & 1
-    want = r_mat * 128 + r_y * 32 + r_zh * 16 + r_x * 4 + r_core * 2 + (r_id & 1)
+    want = ((r_id >> 2) & 3) * 32 + ((r_id >> 1) & 1) * 16 + r_x * 4 + r_core * 2 + (r_id & 1)
     order = jnp.where(s_id == want, 1.0, 0.0).astype(BF16)
     mixers()
     vol_load.wait()
     loads[0].wait()
-    rows[...] = jnp.dot(order, vol[...], preferred_element_type=F32).astype(BF16)
+    for n in range(4):
+        base = ((y + n) % 4) * 32
+        some = jnp.concatenate(
+            [vol[pl.ds(pl.multiple_of(m * 128 + base, 32), 32), :] for m in range(4)], axis=0
+        )
+        some = jnp.dot(order, some, preferred_element_type=F32).astype(BF16)
+        rows[pl.ds(n * 64, 64), :] = some[:64]
+        rows[pl.ds(HALF + n * 64, 64), :] = some[64:]
 
     def turn_block(g, n):
         near = pl.ds(n * 128, 128)
@@ -149,6 +157,15 @@
 
     for n in range(VOX // 128):
         turn_block(0, n)
+
+    def multiply(i):
+        for u in range(2):
+            v = i * 2 + u
+            both = jnp.dot(rows[...], weights[v], preferred_element_type=F32)
+            give[v] = both[:HALF]
+            keep[v] = both[HALF:]
+
+    multiply(0)
     pl.semaphore_wait(barrier, len(peers))
 
     def turn(g):
@@ -239,16 +256,19 @@
     def h_copy(i, d):
         return send(shine.at[i, 1 - d], hrecv.at[i, d], h_s, h_r.at[i], (after, before)[d])
 
+    def hz_copy(n, q, d):
+        owner = (q // 2) * 64 + tile_of(y, q % 2, x, core)
+        return send(
+            hz_out.at[n, pl.ds(q * 16 + (1 - d) * 8, 8)], hz_in.at[n, d, z], hz_s, hz_r.at[n], beside(owner, d)
+        )
+
     def both_views(i):
         return pl.ds(i * 2, 2)
 
     def project(i):
-        for u in range(2):
-            v = i * 2 + u
-            both = jnp.dot(rows[...], weights[v], preferred_element_type=F32)
-            give[v] = both[:HALF]
-            give_copy(v).start()
-            keep[v] = both[HALF:]
+        multiply(i)
+        for u in range(2):
+            give_copy(i * 2 + u).start()
 
     def expand(i):
         await_all(take.at[both_views(i)], core_r.at[i])
@@ -346,17 +366,24 @@
                     zsort[u, pl.ds(32 * k + b, 8, stride=4), :] = part
             for q in range(8):
                 zsend[i, pl.ds(q * 16 + u * 8, 8), :] = zsort[u, pl.ds(q * 8, 8), :]
+
+        @pl.when(i >= PAIRS - DIRECT)
+        def _():
+            n = i - (PAIRS - DIRECT)
+            for q in range(8):
+                for j in range(2):
+                    for u in range(2):
+                        hz_out[n, pl.ds(q * 16 + j * 8 + u * 4, 4), :] = zsort[u, pl.ds(q * 8 + j * 4, 4), :]
+            for d in range(2):
+                for q in range(8):
+                    hz_copy(n, q, d).start()
+
         for d in (4, 3, 5, 2, 6, 1, 7):
             z_copy(i, d).start()
         q = mat * 2 + zh
         zrecv[i, z] = zsend[i, pl.ds(pl.multiple_of(q * 16, 16), 16), :]
 
-    def detect(i):
-        await_all(zrecv.at[i, pl.ds(0, 7)], z_r.at[i])
-        for m in range(MATS):
-            both = zrecv[i, m] + zrecv[i, 4 + m]
-            for u in range(2):
-                proj[pl.ds(m * 8, 8), pl.ds(u * PB, PB)] = both[u * 8 : u * 8 + 8]
+    def expose(keep_at):
         parts = parts_of(proj[...])
         mixed = jnp.concatenate([parts[p] for p in MIX_PROJ], axis=0)
         for j in range(2):
@@ -366,9 +393,31 @@
             second = (bright - first.astype(F32)).astype(BF16)
             large = jnp.dot(resp_mix[...], first, preferred_element_type=F32)
             small = jnp.dot(resp_mix[pl.ds(0, 32), :], second, preferred_element_type=F32)
-            shine[i, j] = large[:32] + (large[32:] + small)
-        h_copy(i, 0).start()
-        h_copy(i, 1).start()
+            keep_at(j)[...] = large[:32] + (large[32:] + small)
+
+    def detect(i):
+        await_all(zrecv.at[i, pl.ds(0, 7)], z_r.at[i])
+        for m in range(MATS):
+            both = zrecv[i, m] + zrecv[i, 4 + m]
+            for u in range(2):
+                proj[pl.ds(m * 8, 8), pl.ds(u * PB, PB)] = both[u * 8 : u * 8 + 8]
+        expose(lambda j: shine.at[i, j])
+
+        @pl.when(i < PAIRS - DIRECT)
+        def _():
+            h_copy(i, 0).start()
+            h_copy(i, 1).start()
+
+        @pl.when(i >= PAIRS - DIRECT)
+        def _():
+            n = i - (PAIRS - DIRECT)
+            await_all(hz_in.at[n], hz_r.at[n])
+            for m in range(MATS):
+                for d in range(2):
+                    proj[pl.ds(m * 8, 8), pl.ds(d * PB, PB)] = hz_in[n, d, m] + hz_in[n, d, 4 + m]
+            expose(lambda j: aside.at[j])
+            for u in range(2):
+                merge(i, u, lambda j, near, u=u: aside[u, near, pl.ds(j * PB, PB)])
 
     share = jnp.zeros((CBINS, PB), F32)
     for n in range(CBINS):
@@ -376,41 +425,58 @@
     rest = 1.0 - 2.0 * share
     outer = (flat > 0, flat < 255)
 
+    def merge(i, u, side_of):
+        half = pl.ds(u * PB, PB)
+        for b in range(4):
+            near = pl.ds(b * 8, 8)
+            own = [shine[i, j, near, half] for j in range(2)]
+            for j in range(2):
+                side = jnp.where(outer[j], side_of(j, near), 0.0)
+                value = rest * own[j] + share * (own[1 - j] + side)
+                obuf[j * 4 + b, pl.ds(i * 2 + u, 8, stride=OPITCH), :] = value
+
     def combine(i):
         await_all(hrecv.at[i], h_r.at[i])
-        for b in range(4):
-            near = pl.ds(b * 8, 8)
-            own = [shine[i, j, near, :] for j in range(2)]
-            for j in range(2):
-                side = jnp.where(outer[j], hrecv[i, j, near, :], 0.0)
-                for u in range(2):
-                    half = slice(u * PB, u * PB + PB)
-                    value = rest * own[j][:, half] + share * (own[1 - j][:, half] + side[:, half])
-                    obuf[j * 4 + b, pl.ds(i * 2 + u, 8, stride=OPITCH), :] = value
+        for u in range(2):
+            merge(i, u, lambda j, near, u=u: hrecv[i, j, near, pl.ds(u * PB, PB)])
+
+    for u in range(2):
+        give_copy(u).start()
+    for r in range(1, 8):
+        pl.semaphore_signal(met, inc=1, device_id=z_peer(r), device_id_type=MESH)
+    project(1)
+    turn(1)
+    expand(0)
 
     stages = (
-        (0, project), (LAG_EXPAND, expand), (LAG_RELAY, pass_on), (LAG_OWNER, gather),
-        (LAG_CROSS, finish), (LAG_DETECT, detect), (LAG_COMBINE, combine),
+        (LAG_PROJECT, 2, PAIRS, project), (LAG_EXPAND, 1, PAIRS, expand), (LAG_RELAY, 0, PAIRS, pass_on),
+        (LAG_OWNER, 0, PAIRS, gather), (LAG_CROSS, 0, PAIRS, finish), (LAG_DETECT, 0, PAIRS, detect),
+        (LAG_COMBINE, 0, PAIRS - DIRECT, combine),
     )
 
     def step(t, carry):
-        for lag, run in stages:
-            i = t - lag
-
-            @pl.when((i >= 0) & (i < PAIRS))
-            def _(i=i, run=run):
-                run(i)
-
+        for lag, first, last, run in stages:
+
+            def reach(n, lag=lag, first=first, last=last):
+                done = n - lag + 1
+                return jnp.where(done > last - MERGE, last, jnp.maximum(done, first))
+
+            lax.fori_loop(reach(t - 1), reach(t), lambda i, c, run=run: (run(i), c)[1], 0)
             if run is project:
-                g = (t // 2) + 1
-
-                @pl.when((t % 2 == 0) & (g < GROUPS))
-                def _(g=g):
-                    turn(g)
+
+                @pl.when((t == 1) | (t == 3))
+                def _():
+                    turn((t + 3) // 2)
+
+            if run is pass_on:
+
+                @pl.when(t == 1)
+                def _():
+                    pl.semaphore_wait(met, 7)
 
         return carry
 
-    lax.fori_loop(0, PAIRS + LAG_COMBINE, step, 0)
+    lax.fori_loop(0, PAIRS + LAG_DETECT, step, 0)
 
     for j in range(2):
         for b in range(4):
@@ -419,7 +485,7 @@
 
     for ref, sem in (
         (give, core_s), (far_out, far_s), (near_out, near_s), (size_out, size_s), (cross_out, cross_s),
-        (csize_out, csize_s), (zsend.at[:, pl.ds(0, 112)], z_s), (shine, h_s),
+        (csize_out, csize_s), (zsend.at[:, pl.ds(0, 112)], z_s), (shine.at[pl.ds(0, PAIRS - DIRECT)], h_s), (hz_out, hz_s),
     ):
         await_all(ref, sem)
 
@@ -464,6 +530,9 @@
             vmem((PAIRS, 2, 32, 2 * PB), F32),
             vmem((PAIRS, 2, 32, 2 * PB), F32),
             vmem((8, CBINS * OPITCH, PB), F32),
+            vmem((DIRECT, 128, PB), F32),
+            vmem((DIRECT, 2, 8, 8, PB), F32),
+            vmem((2, 32, 2 * PB), F32),
             dma((GROUPS + 1,)),
             dma, dma((PAIRS,)),
             dma, dma((PAIRS,)),
@@ -473,9 +542,11 @@
             dma, dma((PAIRS,)),
             dma, dma((PAIRS,)),
             dma, dma((PAIRS,)),
+            dma, dma((DIRECT,)),
+            pltpu.SemaphoreType.REGULAR,
         ],
         compiler_params=pltpu.CompilerParams(
-            collective_id=0, has_side_effects=True, vmem_limit_bytes=67043328
+            collective_id=0, has_side_effects=True, vmem_limit_bytes=56 * 2**20
         ),
     )(
         volume.reshape(SLICES, VOX),

time: 64.7 us -> 60.2 us (0.930)
  Pallas kernels: 62.6 us -> 58.1 us
    pallas_call x1, Pallas kernels: 62.6 us -> 58.1 us  [per_device(): pl.pallas_call(kernel, out_shape=jax.ShapeDtypeStruct((CBINS, 2, VIEWS, P...]
where the time goes in v3:
time: 60.2 us; the launch traced here: 60 us
  Pallas kernels  58.1 us (97%)
  local copies, waits for them, and re-layouts  1.88 us (3%)
    pallas_call x1, Pallas kernels, per_device(): pl.pallas_call(kernel, out_shape=jax.ShapeDtypeStruct((CBINS, 2, VIEWS, P...  58.1 us
    unnamed x1, local copies, waits for them, and re-layouts  1.88 us

profile of v3, /device:TPU:32, one launch (start us, length us, event | category | flops | bytes accessed | tf_op | source)
XLA Modules:
  0.0 60.0 jit_solution(5519708959711573920)
XLA Ops:
  0.0 58.1 %shard_map.64 = f32[8,2,16,512]{3,2,1,0:T(8,128)} custom-call(bf16[512,1024]{1,0:T(8,128)(2,1)} %bitcast.4, bf16[1024,32,128]{2,1,0:T(8,128)(2,1)} %bitcast.3, s32[16,64]{1,0:T(8,128)} %bitcast.5, f32[4,64]{1,0:T(4,128)} %att.1, f32[8,64]{1,0:T(8,128)} %resp.1, f32[8]{0:T(128)} %leak.1), custom_call_target="tpu_custom_call" | custom-call | tf_op jit(solution)/shard_map/pallas_call | solution.py:499
  58.1 1.9 %copy.8 = f32[8,2,16,512]{3,2,1,0:T(8,128)} copy(f32[8,2,16,512]{3,2,1,0:T(8,128)} %shard_map.64) | data formatting | bytes 1048576

commit v4 on v3

--- a/solution.py
+++ b/solution.py
@@ -34,10 +34,8 @@
 LAG_OWNER = 2
 LAG_CROSS = 3
 LAG_DETECT = 5
-LAG_COMBINE = 7
 MERGE = 2
 OPITCH = 24
-DIRECT = 2
 
 
 def kernel(
@@ -47,9 +45,9 @@
     give, keep, take,
     ext, far_out, far_in, near_out, near_in, size_out, size_in,
     owned, cross_out, cross_in, csize_out, csize_in,
-    zsort, zsend, zrecv, proj, att_mix, resp_mix, shine, hrecv, obuf, hz_out, hz_in, aside,
+    zsort, deep_out, deep_in, side_in, dsize_out, dsize_in, ssize_in, proj, att_mix, resp_mix, shine, aside, obuf,
     load_sem, core_s, core_r, far_s, far_r, near_s, near_r, size_s, size0_r, size1_r,
-    cross_s, cross_r, csize_s, csize_r, z_s, z_r, h_s, h_r, hz_s, hz_r, met,
+    cross_s, cross_r, csize_s, csize_r, deep_s, deep_r, side_s, side_r, dsize_s, dsize_r, ssize_s, ssize_r, met,
 ):
     mat = lax.axis_index("mat")
     tile = lax.axis_index("tile")
@@ -242,24 +240,20 @@
     def lanes(b):
         return pl.ds(b * PB, PB)
 
-    def z_copy(i, d):
+    def deep_pair(i, d):
         zt = (z + d) % 8
         q = (zt % 4) * 2 + zt // 4
-        return send(
-            zsend.at[i, pl.ds(pl.multiple_of(q * 16, 16), 16)],
-            zrecv.at[i, z],
-            z_s,
-            z_r.at[i],
-            z_peer(d),
-        )
-
-    def h_copy(i, d):
-        return send(shine.at[i, 1 - d], hrecv.at[i, d], h_s, h_r.at[i], (after, before)[d])
-
-    def hz_copy(n, q, d):
+        return (
+            send(deep_out.at[i, q], deep_in.at[i, z], deep_s, deep_r.at[i], z_peer(d)),
+            send(dsize_out.at[i], dsize_in.at[i, z], dsize_s, dsize_r.at[i], z_peer(d)),
+        )
+
+    def side_pair(i, q, d):
         owner = (q // 2) * 64 + tile_of(y, q % 2, x, core)
-        return send(
-            hz_out.at[n, pl.ds(q * 16 + (1 - d) * 8, 8)], hz_in.at[n, d, z], hz_s, hz_r.at[n], beside(owner, d)
+        peer = beside(owner, d)
+        return (
+            send(deep_out.at[i, q, 1 - d], side_in.at[i, d, z], side_s, side_r.at[i], peer),
+            send(dsize_out.at[i], ssize_in.at[i, d, z], ssize_s, ssize_r.at[i], peer),
         )
 
     def both_views(i):
@@ -364,26 +358,23 @@
                 for k in range(2):
                     part = owned[v, pl.ds(8 * k, 8), lanes(b)] + (got[0][k] + (got[1][k] + got[2][k]))
                     zsort[u, pl.ds(32 * k + b, 8, stride=4), :] = part
+        top = peak(zsort[u, pl.ds(8 * n, 8), :] for u in range(2) for n in range(8))
+        dsize_out[i] = top * (1.0 / TOP)
+        word = code(zsort[0], zsort[1], inverse_of(top))
+        for q in range(8):
+            for j in range(2):
+                deep_out[i, q, j] = word[q * 8 + j * 4 : q * 8 + j * 4 + 4]
+        for d in range(2):
             for q in range(8):
-                zsend[i, pl.ds(q * 16 + u * 8, 8), :] = zsort[u, pl.ds(q * 8, 8), :]
-
-        @pl.when(i >= PAIRS - DIRECT)
-        def _():
-            n = i - (PAIRS - DIRECT)
-            for q in range(8):
-                for j in range(2):
-                    for u in range(2):
-                        hz_out[n, pl.ds(q * 16 + j * 8 + u * 4, 4), :] = zsort[u, pl.ds(q * 8 + j * 4, 4), :]
-            for d in range(2):
-                for q in range(8):
-                    hz_copy(n, q, d).start()
-
+                for copy in side_pair(i, q, d):
+                    copy.start()
         for d in (4, 3, 5, 2, 6, 1, 7):
-            z_copy(i, d).start()
-        q = mat * 2 + zh
-        zrecv[i, z] = zsend[i, pl.ds(pl.multiple_of(q * 16, 16), 16), :]
-
-    def expose(keep_at):
+            for copy in deep_pair(i, d):
+                copy.start()
+        deep_in[i, z] = deep_out[i, mat * 2 + zh]
+        dsize_in[i, z] = dsize_out[i]
+
+    def expose(target):
         parts = parts_of(proj[...])
         mixed = jnp.concatenate([parts[p] for p in MIX_PROJ], axis=0)
         for j in range(2):
@@ -393,52 +384,41 @@
             second = (bright - first.astype(F32)).astype(BF16)
             large = jnp.dot(resp_mix[...], first, preferred_element_type=F32)
             small = jnp.dot(resp_mix[pl.ds(0, 32), :], second, preferred_element_type=F32)
-            keep_at(j)[...] = large[:32] + (large[32:] + small)
+            target[j] = large[:32] + (large[32:] + small)
 
     def detect(i):
-        await_all(zrecv.at[i, pl.ds(0, 7)], z_r.at[i])
+        await_all(dsize_in.at[i, pl.ds(0, 7)], dsize_r.at[i])
+        await_all(deep_in.at[i, pl.ds(0, 7)], deep_r.at[i])
         for m in range(MATS):
-            both = zrecv[i, m] + zrecv[i, 4 + m]
+            for j in range(2):
+                one = decode(deep_in[i, m, j], dsize_in[i, m])
+                two = decode(deep_in[i, 4 + m, j], dsize_in[i, 4 + m])
+                for u in range(2):
+                    proj[pl.ds(m * 8 + j * 4, 4), lanes(u)] = one[u] + two[u]
+        expose(shine)
+        await_all(ssize_in.at[i], ssize_r.at[i])
+        await_all(side_in.at[i], side_r.at[i])
+        for m in range(MATS):
+            for d in range(2):
+                one = decode(side_in[i, d, m], ssize_in[i, d, m])
+                two = decode(side_in[i, d, 4 + m], ssize_in[i, d, 4 + m])
+                for u in range(2):
+                    proj[pl.ds(m * 8 + d * 4, 4), lanes(u)] = one[u] + two[u]
+        expose(aside)
+        for b in range(4):
+            near = pl.ds(b * 8, 8)
             for u in range(2):
-                proj[pl.ds(m * 8, 8), pl.ds(u * PB, PB)] = both[u * 8 : u * 8 + 8]
-        expose(lambda j: shine.at[i, j])
-
-        @pl.when(i < PAIRS - DIRECT)
-        def _():
-            h_copy(i, 0).start()
-            h_copy(i, 1).start()
-
-        @pl.when(i >= PAIRS - DIRECT)
-        def _():
-            n = i - (PAIRS - DIRECT)
-            await_all(hz_in.at[n], hz_r.at[n])
-            for m in range(MATS):
-                for d in range(2):
-                    proj[pl.ds(m * 8, 8), pl.ds(d * PB, PB)] = hz_in[n, d, m] + hz_in[n, d, 4 + m]
-            expose(lambda j: aside.at[j])
-            for u in range(2):
-                merge(i, u, lambda j, near, u=u: aside[u, near, pl.ds(j * PB, PB)])
+                own = [shine[j, near, lanes(u)] for j in range(2)]
+                for j in range(2):
+                    side = jnp.where(outer[j], aside[j, near, lanes(u)], 0.0)
+                    value = rest * own[j] + share * (own[1 - j] + side)
+                    obuf[j * 4 + b, pl.ds(i * 2 + u, 8, stride=OPITCH), :] = value
 
     share = jnp.zeros((CBINS, PB), F32)
     for n in range(CBINS):
         share = jnp.where(iota((CBINS, PB), 0) == n, leak[n], share)
     rest = 1.0 - 2.0 * share
     outer = (flat > 0, flat < 255)
-
-    def merge(i, u, side_of):
-        half = pl.ds(u * PB, PB)
-        for b in range(4):
-            near = pl.ds(b * 8, 8)
-            own = [shine[i, j, near, half] for j in range(2)]
-            for j in range(2):
-                side = jnp.where(outer[j], side_of(j, near), 0.0)
-                value = rest * own[j] + share * (own[1 - j] + side)
-                obuf[j * 4 + b, pl.ds(i * 2 + u, 8, stride=OPITCH), :] = value
-
-    def combine(i):
-        await_all(hrecv.at[i], h_r.at[i])
-        for u in range(2):
-            merge(i, u, lambda j, near, u=u: hrecv[i, j, near, pl.ds(u * PB, PB)])
 
     for u in range(2):
         give_copy(u).start()
@@ -451,7 +431,6 @@
     stages = (
         (LAG_PROJECT, 2, PAIRS, project), (LAG_EXPAND, 1, PAIRS, expand), (LAG_RELAY, 0, PAIRS, pass_on),
         (LAG_OWNER, 0, PAIRS, gather), (LAG_CROSS, 0, PAIRS, finish), (LAG_DETECT, 0, PAIRS, detect),
-        (LAG_COMBINE, 0, PAIRS - DIRECT, combine),
     )
 
     def step(t, carry):
@@ -485,7 +464,8 @@
 
     for ref, sem in (
         (give, core_s), (far_out, far_s), (near_out, near_s), (size_out, size_s), (cross_out, cross_s),
-        (csize_out, csize_s), (zsend.at[:, pl.ds(0, 112)], z_s), (shine.at[pl.ds(0, PAIRS - DIRECT)], h_s), (hz_out, hz_s),
+        (csize_out, csize_s), (deep_out.at[:, pl.ds(0, 7)], deep_s), (side_in, side_s),
+        (dsize_in.at[:, pl.ds(0, 7)], dsize_s), (ssize_in, ssize_s),
     ):
         await_all(ref, sem)
 
@@ -522,17 +502,18 @@
             vmem((VIEWS, 3, 1, PB), F32),
             vmem((VIEWS, 3, 1, PB), F32),
             vmem((2, 64, PB), F32),
-            vmem((PAIRS, 128, PB), F32),
-            vmem((PAIRS, 8, 16, PB), F32),
+            vmem((PAIRS, 8, 2, 4, PB), I32),
+            vmem((PAIRS, 8, 2, 4, PB), I32),
+            vmem((PAIRS, 2, 8, 4, PB), I32),
+            vmem((PAIRS, 1, PB), F32),
+            vmem((PAIRS, 8, 1, PB), F32),
+            vmem((PAIRS, 2, 8, 1, PB), F32),
             vmem((32, 2 * PB), F32),
             vmem((8 * EBINS, len(MIX_ATT) * 32), BF16),
             vmem((64, 256), BF16),
-            vmem((PAIRS, 2, 32, 2 * PB), F32),
-            vmem((PAIRS, 2, 32, 2 * PB), F32),
+            vmem((2, 32, 2 * PB), F32),
+            vmem((2, 32, 2 * PB), F32),
             vmem((8, CBINS * OPITCH, PB), F32),
-            vmem((DIRECT, 128, PB), F32),
-            vmem((DIRECT, 2, 8, 8, PB), F32),
-            vmem((2, 32, 2 * PB), F32),
             dma((GROUPS + 1,)),
             dma, dma((PAIRS,)),
             dma, dma((PAIRS,)),
@@ -542,7 +523,8 @@
             dma, dma((PAIRS,)),
             dma, dma((PAIRS,)),
             dma, dma((PAIRS,)),
-            dma, dma((DIRECT,)),
+            dma, dma((PAIRS,)),
+            dma, dma((PAIRS,)),
             pltpu.SemaphoreType.REGULAR,
         ],
         compiler_params=pltpu.CompilerParams(

time: 60.2 us -> 56 us (0.930)
  the two profiles are of different devices: /device:TPU:32 before, /device:TPU:1 now
where the time goes in v4:
time: 56 us; the launch traced here: 55.8 us
  Pallas kernels  53.9 us (96%)
  local copies, waits for them, and re-layouts  1.88 us (3%)
    pallas_call x1, Pallas kernels, per_device(): pl.pallas_call(kernel, out_shape=jax.ShapeDtypeStruct((CBINS, 2, VIEWS, P...  53.9 us
    unnamed x1, local copies, waits for them, and re-layouts  1.88 us

profile of v4, /device:TPU:1, one launch (start us, length us, event | category | flops | bytes accessed | tf_op | source)
XLA Modules:
  0.0 55.8 jit_solution(2515009841739513995)
XLA Ops:
  0.0 53.9 %shard_map.64 = f32[8,2,16,512]{3,2,1,0:T(8,128)} custom-call(bf16[512,1024]{1,0:T(8,128)(2,1)} %bitcast.4, bf16[1024,32,128]{2,1,0:T(8,128)(2,1)} %bitcast.3, s32[16,64]{1,0:T(8,128)} %bitcast.5, f32[4,64]{1,0:T(4,128)} %att.1, f32[8,64]{1,0:T(8,128)} %resp.1, f32[8]{0:T(128)} %leak.1), custom_call_target="tpu_custom_call" | custom-call | tf_op jit(solution)/shard_map/pallas_call | solution.py:479
  53.9 1.9 %copy.8 = f32[8,2,16,512]{3,2,1,0:T(8,128)} copy(f32[8,2,16,512]{3,2,1,0:T(8,128)} %shard_map.64) | data formatting | bytes 1048576

commit v5 on v4

--- a/solution.py
+++ b/solution.py
@@ -31,10 +31,9 @@
 LAG_PROJECT = -2
 LAG_EXPAND = -1
 LAG_RELAY = 1
-LAG_OWNER = 2
-LAG_CROSS = 3
-LAG_DETECT = 5
-MERGE = 2
+LAG_OWNER = 3
+LAG_CROSS = 4
+LAG_DETECT = 6
 OPITCH = 24
 
 
@@ -429,16 +428,16 @@
     expand(0)
 
     stages = (
-        (LAG_PROJECT, 2, PAIRS, project), (LAG_EXPAND, 1, PAIRS, expand), (LAG_RELAY, 0, PAIRS, pass_on),
-        (LAG_OWNER, 0, PAIRS, gather), (LAG_CROSS, 0, PAIRS, finish), (LAG_DETECT, 0, PAIRS, detect),
+        (LAG_PROJECT, 2, 2, project), (LAG_EXPAND, 1, 2, expand), (LAG_RELAY, 0, 3, pass_on),
+        (LAG_OWNER, 0, 4, gather), (LAG_CROSS, 0, 2, finish), (LAG_DETECT, 0, 3, detect),
     )
 
     def step(t, carry):
-        for lag, first, last, run in stages:
-
-            def reach(n, lag=lag, first=first, last=last):
+        for lag, first, merge, run in stages:
+
+            def reach(n, lag=lag, first=first, merge=merge):
                 done = n - lag + 1
-                return jnp.where(done > last - MERGE, last, jnp.maximum(done, first))
+                return jnp.where(done > PAIRS - merge, PAIRS, jnp.maximum(done, first))
 
             lax.fori_loop(reach(t - 1), reach(t), lambda i, c, run=run: (run(i), c)[1], 0)
             if run is project:
@@ -455,7 +454,7 @@
 
         return carry
 
-    lax.fori_loop(0, PAIRS + LAG_DETECT, step, 0)
+    lax.fori_loop(0, PAIRS + LAG_DETECT - 2, step, 0)
 
     for j in range(2):
         for b in range(4):
@@ -478,7 +477,7 @@
     near = pl.BlockSpec(memory_space=pltpu.VMEM)
     return pl.pallas_call(
         kernel,
-        out_shape=jax.ShapeDtypeStruct((CBINS, 2, VIEWS, PIX), F32),
+        out_shape=pltpu.VMEM((CBINS, 2, VIEWS, PIX), F32),
         in_specs=[far, far, smem, near, near, smem],
         out_specs=pl.BlockSpec(memory_space=pltpu.VMEM),
         scratch_shapes=[

time: 56 us -> 54.4 us (0.971)
  the two profiles are of different devices: /device:TPU:1 before, /device:TPU:32 now
where the time goes in v5:
time: 54.4 us; the launch traced here: 54.3 us
  Pallas kernels  53.5 us (98%)
  local copies, waits for them, and re-layouts  0.8 us (1%)
    pallas_call x1, Pallas kernels, per_device(): pl.pallas_call(kernel, out_shape=pltpu.VMEM((CBINS, 2, VIEWS, PIX), F32),...  53.5 us

profile of v5, /device:TPU:32, one launch (start us, length us, event | category | flops | bytes accessed | tf_op | source)
XLA Modules:
  0.0 54.3 jit_solution(3741140618801189567)
XLA Ops:
  0.0 53.5 %shard_map.64 = f32[8,2,16,512]{3,2,1,0:T(8,128)S(1)} custom-call(bf16[512,1024]{1,0:T(8,128)(2,1)} %bitcast.4, bf16[1024,32,128]{2,1,0:T(8,128)(2,1)} %bitcast.3, s32[16,64]{1,0:T(8,128)} %bitcast.5, f32[4,64]{1,0:T(4,128)} %att.1, f32[8,64]{1,0:T(8,128)} %resp.1, f32[8]{0:T(128)} %leak.1), custom_call_target="tpu_custom_call" | custom-call | tf_op jit(solution)/shard_map/pallas_call | solution.py:478
  53.5 0.8 %copy.8 = f32[8,2,16,512]{3,2,1,0:T(8,128)} copy(f32[8,2,16,512]{3,2,1,0:T(8,128)S(1)} %shard_map.64) | data formatting | bytes 1048576
